TPU v7x, 32 devices: a whole 2x2x4 slice. The times are simulated.
32 devices in a mesh: seq: 8 (over y, x, core), rep: 4 (over z).
Axes of the slice: x: 2, y: 2, z: 4, core: 2. Of those that a mesh axis runs over, the one named last changes fastest.
Arguments:
- prefix_cache: bfloat16 [2, 2, 1024, 4096], P(None, None, 'seq', 'rep'), may hold values from -5 to 5
- queries: bfloat16 [2, 32, 4096], P(None, ('seq', 'rep')), may hold values from -12 to 12
- suffix_cache: bfloat16 [2, 32, 2, 128, 1024], P(None, ('seq', 'rep')), may hold values from -9 to 9
- suffix_lengths: int32 [32], replicated, may hold values from 1 to 128, as said below
- slot_request: int32 [32], P(('seq', 'rep')), may hold values from 0 to 31, each once
Outputs:
- attended: bfloat16 [2, 32, 4096], P(None, ('seq', 'rep'))
Inputs may be any that keep to these rules, and one draw needn't show every extreme that they name: `suffix_lengths`: every request has 1 to 128 suffix tokens; some request has exactly 128. `slot_request`: every request id stands in exactly one slot.
All inputs are finite; a program needn't handle non-finite values.
Results may differ from a plain program's by a relative error of at most 0.005.
Values may be sent and summed in bfloat16 or wider, within the bound.
A program may use at most 64 MiB of HBM per device.

v0:
```python
import jax
import jax.numpy as jnp
from jax import lax
from jax.sharding import PartitionSpec as P

QH = 32
KVH = 8
HD = 128
SUF = 128
GROUP = 4


neg_fill = -1e30


def body(prefix_cache, queries, suffix_cache, suffix_lengths, slot_request):
    layer_total = queries.shape[0]
    own_rows = queries.shape[1]
    score_scale = HD ** (-0.5)
    request_table = jnp.arange(suffix_lengths.shape[0], dtype=jnp.int32)
    lengths = jnp.sum(
        jnp.where(slot_request[:, None] == request_table[None, :], suffix_lengths[None, :], 0),
        axis=1,
    )
    valid_mask = (jnp.arange(SUF, dtype=jnp.int32)[None, :] < lengths[:, None])[:, None, None, :]
    gathered = lax.all_gather(queries, "seq", axis=1, tiled=True)
    results = []
    for layer_index in range(layer_total):
        moved_layer = lax.all_to_all(
            prefix_cache[layer_index], "seq", split_axis=2, concat_axis=1, tiled=True
        )
        kv_block = lax.all_gather(moved_layer, "rep", axis=2, tiled=True)
        query_rows = gathered[layer_index]
        row_count = query_rows.shape[0]
        positions = kv_block.shape[2]
        shaped = query_rows.reshape(row_count, KVH, GROUP, HD)
        key_block = kv_block[0].reshape(KVH, HD, positions)
        value_block = kv_block[1].reshape(KVH, HD, positions)
        scores = (
            jnp.einsum("rhgd,hdp->rhgp", shaped, key_block, preferred_element_type=jnp.float32)
            * score_scale
        )
        local_top = jnp.max(scores, axis=3)
        weights = jnp.exp(scores - local_top[..., None]).astype(jnp.bfloat16)
        numerator = jnp.einsum(
            "rhgp,hdp->rhgd", weights, value_block, preferred_element_type=jnp.float32
        ).reshape(row_count, 1, QH * HD)
        denominator = jnp.sum(weights, axis=3, dtype=jnp.float32).reshape(row_count, 1, QH)
        source_tops = local_top.reshape(row_count, 1, QH)
        arrived = (
            lax.all_to_all(numerator, "seq", split_axis=0, concat_axis=1, tiled=True),
            lax.all_to_all(denominator, "seq", split_axis=0, concat_axis=1, tiled=True),
            lax.all_to_all(source_tops, "seq", split_axis=0, concat_axis=1, tiled=True),
        )
        own_top = jnp.max(arrived[2], axis=1)
        factor = jnp.exp(arrived[2] - own_top[:, None, :])
        sources = arrived[0].shape[1]
        prefix_num = jnp.sum(
            arrived[0].reshape(own_rows, sources, QH, HD) * factor[..., None], axis=1
        ).reshape(own_rows, QH * HD)
        prefix_den = jnp.sum(arrived[1] * factor, axis=1)
        own_queries = queries[layer_index].reshape(own_rows, KVH, GROUP, HD)
        suffix_keys = suffix_cache[layer_index, :, 0].reshape(own_rows, SUF, KVH, HD)
        suffix_values = suffix_cache[layer_index, :, 1].reshape(own_rows, SUF, KVH, HD)
        suffix_scores = (
            jnp.einsum(
                "rhgd,rshd->rhgs", own_queries, suffix_keys, preferred_element_type=jnp.float32
            )
            * score_scale
        )
        suffix_scores = jnp.where(valid_mask, suffix_scores, neg_fill)
        suffix_top = jnp.max(suffix_scores, axis=3)
        suffix_weights = jnp.where(
            valid_mask, jnp.exp(suffix_scores - suffix_top[..., None]), 0.0
        ).astype(jnp.bfloat16)
        suffix_num = jnp.einsum(
            "rhgs,rshd->rhgd", suffix_weights, suffix_values, preferred_element_type=jnp.float32
        ).reshape(own_rows, QH, HD)
        suffix_den = jnp.sum(suffix_weights, axis=3, dtype=jnp.float32).reshape(own_rows, QH)
        suffix_top = suffix_top.reshape(own_rows, QH)
        both_top = jnp.maximum(own_top, suffix_top)
        prefix_scale = jnp.exp(own_top - both_top)
        suffix_scale = jnp.exp(suffix_top - both_top)
        total_den = prefix_scale * prefix_den + suffix_scale * suffix_den
        mixed = (
            prefix_scale[..., None] * prefix_num.reshape(own_rows, QH, HD)
            + suffix_scale[..., None] * suffix_num
        ) / total_den[..., None]
        results.append(mixed.reshape(own_rows, QH * HD).astype(jnp.bfloat16))
    return jnp.stack(results)


def solution(mesh):
    in_specs = (
        P(None, None, "seq", "rep"),
        P(None, ("seq", "rep"), None),
        P(None, ("seq", "rep"), None, None, None),
        P(),
        P(("seq", "rep")),
    )
    out_specs = P(None, ("seq", "rep"), None)
    return jax.shard_map(body, mesh=mesh, in_specs=in_specs, out_specs=out_specs, check_vma=False)
```

profile of v0, /device:TPU:0, one launch (start us, length us, event | category | flops | bytes accessed | tf_op | source)
XLA Modules:
  0.0 172.0 jit_solution(15740848933637887139)
XLA Ops:
  6.5 1.3 fusion.28
  8.2 14.7 %all_to_all.108 = bf16[2,128,1024]{1,0,2:T(2,128)(2,1)S(1)} all-to-all(bf16[2,128,1024]{1,0,2:T(2,128)(2,1)S(1)} %bitcast.112), channel_id=1, replica_groups=mesh['seq'=8,'rep'=4] {'seq'}, dimensions={2} | all-to-all | bytes 1048576 | tf_op jit(solution)/shard_map/all_to_all | solution.py:29
  22.9 1.1 copy.47
  24.5 12.1 %all_to_all.109 = bf16[2,128,1024]{1,0,2:T(2,128)(2,1)S(1)} all-to-all(bf16[2,128,1024]{1,0,2:T(2,128)(2,1)S(1)} %bitcast.114), channel_id=1, replica_groups=mesh['seq'=8,'rep'=4] {'seq'}, dimensions={2} | all-to-all | bytes 1048576 | tf_op jit(solution)/shard_map/all_to_all | solution.py:29
  36.7 1.1 copy.58
  38.9 0.7 fusion.18
  39.6 0.6 iota_compare_fusion
  41.7 8.3 %all_gather.10 = bf16[2,8,4096]{2,0,1:T(2,128)(2,1)S(1)} all-gather(bf16[2,1,4096]{2,0,1:T(2,128)(2,1)S(1)} %copy-done.1), channel_id=1, replica_groups=mesh['seq'=8,'rep'=4] {'seq'}, dimensions={1}, use_global_device_ids=true | all-gather | bytes 147456 | tf_op jit(solution)/shard_map/all_gather | solution.py:26
  50.0 0.6 slice_reduce_fusion.1
  51.1 18.8 %all-gather.3.cloned.1.call-done = bf16[2,1024,512]{2,1,0:T(8,128)(2,1)} async-done(((bf16[2,1024,128]{2,1,0:T(8,128)(2,1)}), bf16[2,1024,512]{2,1,0:T(8,128)(2,1)}) %all-gather.3.cloned.1.call-update) | async-done | bytes 2097168 | tf_op jit(solution)/shard_map/all_gather | solution.py:32
  69.8 1.7 fusion.25
  71.9 0.7 copy.49
  72.5 3.7 %all-to-all-start.1 = ((f32[8,1,32]{2,1,0:T(1,128)}), f32[8,1,32]{2,1,0:T(1,128)S(1)}, u32[]{:S(2)}, u32[]{:S(2)}) async-start(f32[8,1,32]{2,1,0:T(1,128)} %copy.49), calls=%async_computation.1 | async-start | bytes 8192 | tf_op jit(solution)/shard_map/all_to_all | solution.py:53
  76.5 0.5 fusion.4
  76.9 38.9 %all-gather.5.cloned.1.call-done = bf16[2,1024,512]{2,1,0:T(8,128)(2,1)} async-done(((bf16[2,1024,128]{2,1,0:T(8,128)(2,1)}), bf16[2,1024,512]{2,1,0:T(8,128)(2,1)}) %all-gather.5.cloned.1.call-update) | async-done | bytes 2097168 | tf_op jit(solution)/shard_map/all_gather | solution.py:32
  115.9 1.7 fusion.26
  118.7 0.7 copy.56
  119.3 0.8 copy.52
  120.1 0.7 copy.67
  120.8 0.8 copy.63
  121.6 0.7 copy.60
  122.2 3.7 %all-to-all-start.5 = ((f32[8,1,32]{2,1,0:T(1,128)}), f32[8,1,32]{2,1,0:T(1,128)S(1)}, u32[]{:S(2)}, u32[]{:S(2)}) async-start(f32[8,1,32]{2,1,0:T(1,128)} %copy.60), calls=%async_computation.5 | async-start | bytes 8192 | tf_op jit(solution)/shard_map/all_to_all | solution.py:53
  125.9 4.6 %all-to-all-done.5 = f32[8,1,32]{2,1,0:T(1,128)S(1)} async-done(((f32[8,1,32]{2,1,0:T(1,128)}), f32[8,1,32]{2,1,0:T(1,128)S(1)}, u32[]{:S(2)}, u32[]{:S(2)}) %all-to-all-start.5) | async-done | bytes 1056 | tf_op jit(solution)/shard_map/all_to_all | solution.py:53
  130.5 3.3 %all-to-all-start.3 = ((f32[8,1,32]{2,1,0:T(1,128)}), f32[8,1,32]{2,1,0:T(1,128)S(1)}, u32[]{:S(2)}, u32[]{:S(2)}) async-start(f32[8,1,32]{2,1,0:T(1,128)} %copy.56), calls=%async_computation.3 | async-start | bytes 8192 | tf_op jit(solution)/shard_map/all_to_all | solution.py:52
  133.8 4.6 %all-to-all-done.3 = f32[8,1,32]{2,1,0:T(1,128)S(1)} async-done(((f32[8,1,32]{2,1,0:T(1,128)}), f32[8,1,32]{2,1,0:T(1,128)S(1)}, u32[]{:S(2)}, u32[]{:S(2)}) %all-to-all-start.3) | async-done | bytes 1056 | tf_op jit(solution)/shard_map/all_to_all | solution.py:52
  138.4 3.3 %all-to-all-start.7 = ((f32[8,1,32]{2,1,0:T(1,128)}), f32[8,1,32]{2,1,0:T(1,128)S(1)}, u32[]{:S(2)}, u32[]{:S(2)}) async-start(f32[8,1,32]{2,1,0:T(1,128)} %copy.67), calls=%async_computation.7 | async-start | bytes 8192 | tf_op jit(solution)/shard_map/all_to_all | solution.py:52
  141.7 4.6 %all-to-all-done.7 = f32[8,1,32]{2,1,0:T(1,128)S(1)} async-done(((f32[8,1,32]{2,1,0:T(1,128)}), f32[8,1,32]{2,1,0:T(1,128)S(1)}, u32[]{:S(2)}, u32[]{:S(2)}) %all-to-all-start.7) | async-done | bytes 1056 | tf_op jit(solution)/shard_map/all_to_all | solution.py:52
  146.3 3.4 %all-to-all-start.2 = ((f32[8,1,4096]{2,1,0:T(1,128)}), f32[8,1,4096]{2,1,0:T(1,128)S(1)}, u32[]{:S(2)}, u32[]{:S(2)}) async-start(f32[8,1,4096]{2,1,0:T(1,128)} %copy.52), calls=%async_computation.2 | async-start | bytes 262144 | tf_op jit(solution)/shard_map/all_to_all | solution.py:51
  149.8 5.4 %all-to-all-done.2 = f32[8,1,4096]{2,1,0:T(1,128)S(1)} async-done(((f32[8,1,4096]{2,1,0:T(1,128)}), f32[8,1,4096]{2,1,0:T(1,128)S(1)}, u32[]{:S(2)}, u32[]{:S(2)}) %all-to-all-start.2) | async-done | bytes 131104 | tf_op jit(solution)/shard_map/all_to_all | solution.py:51
  155.1 3.4 %all-to-all-start.6 = ((f32[8,1,4096]{2,1,0:T(1,128)}), f32[8,1,4096]{2,1,0:T(1,128)S(1)}, u32[]{:S(2)}, u32[]{:S(2)}) async-start(f32[8,1,4096]{2,1,0:T(1,128)} %copy.63), calls=%async_computation.6 | async-start | bytes 262144 | tf_op jit(solution)/shard_map/all_to_all | solution.py:51
  159.0 4.9 %all-to-all-done.6 = f32[8,1,4096]{2,1,0:T(1,128)S(1)} async-done(((f32[8,1,4096]{2,1,0:T(1,128)}), f32[8,1,4096]{2,1,0:T(1,128)S(1)}, u32[]{:S(2)}, u32[]{:S(2)}) %all-to-all-start.6) | async-done | bytes 131104 | tf_op jit(solution)/shard_map/all_to_all | solution.py:51
  164.5 0.6 pad_maximum_fusion
  (53 shorter events, 6.2 us)
Async XLA Ops:
  6.5 63.3 %all-gather.3.cloned.1.call-start = ((), (), s32[]{:S(2)}) async-start(), calls=%async_computation.8 | async-start | bytes 2621440 | tf_op jit(solution)/shard_map/all_gather | solution.py:32
  24.0 14.4 %copy-start = (bf16[2,1,2,128,1024]{4,3,2,1,0:T(8,128)(2,1)S(1)}, bf16[2,1,2,128,1024]{4,3,2,1,0:T(8,128)(2,1)}, u32[]{:S(2)}) copy-start(bf16[2,1,2,128,1024]{4,3,2,1,0:T(8,128)(2,1)} %param.7) | copy-start | bytes 3145732
  24.1 91.8 %all-gather.5.cloned.1.call-start = ((), (), s32[]{:S(2)}) async-start(), calls=%async_computation.9 | async-start | bytes 2621440 | tf_op jit(solution)/shard_map/all_gather | solution.py:32
  37.8 1.1 copy-start.2
  37.8 2.4 %copy-start.1 = (bf16[2,1,4096]{2,0,1:T(2,128)(2,1)S(1)}, bf16[2,1,4096]{2,0,1:T(2,128)(2,1)}, u32[]{:S(2)}) copy-start(bf16[2,1,4096]{2,0,1:T(2,128)(2,1)} %param.6) | copy-start | bytes 49156
  72.5 49.7 %all-to-all-start.1 = ((f32[8,1,32]{2,1,0:T(1,128)}), f32[8,1,32]{2,1,0:T(1,128)S(1)}, u32[]{:S(2)}, u32[]{:S(2)}) async-start(f32[8,1,32]{2,1,0:T(1,128)} %copy.49), calls=%async_computation.1 | async-start | bytes 8192 | tf_op jit(solution)/shard_map/all_to_all | solution.py:53
  122.2 8.3 %all-to-all-start.5 = ((f32[8,1,32]{2,1,0:T(1,128)}), f32[8,1,32]{2,1,0:T(1,128)S(1)}, u32[]{:S(2)}, u32[]{:S(2)}) async-start(f32[8,1,32]{2,1,0:T(1,128)} %copy.60), calls=%async_computation.5 | async-start | bytes 8192 | tf_op jit(solution)/shard_map/all_to_all | solution.py:53
  130.5 7.9 %all-to-all-start.3 = ((f32[8,1,32]{2,1,0:T(1,128)}), f32[8,1,32]{2,1,0:T(1,128)S(1)}, u32[]{:S(2)}, u32[]{:S(2)}) async-start(f32[8,1,32]{2,1,0:T(1,128)} %copy.56), calls=%async_computation.3 | async-start | bytes 8192 | tf_op jit(solution)/shard_map/all_to_all | solution.py:52
  138.4 7.9 %all-to-all-start.7 = ((f32[8,1,32]{2,1,0:T(1,128)}), f32[8,1,32]{2,1,0:T(1,128)S(1)}, u32[]{:S(2)}, u32[]{:S(2)}) async-start(f32[8,1,32]{2,1,0:T(1,128)} %copy.67), calls=%async_computation.7 | async-start | bytes 8192 | tf_op jit(solution)/shard_map/all_to_all | solution.py:52
  146.3 8.8 %all-to-all-start.2 = ((f32[8,1,4096]{2,1,0:T(1,128)}), f32[8,1,4096]{2,1,0:T(1,128)S(1)}, u32[]{:S(2)}, u32[]{:S(2)}) async-start(f32[8,1,4096]{2,1,0:T(1,128)} %copy.52), calls=%async_computation.2 | async-start | bytes 262144 | tf_op jit(solution)/shard_map/all_to_all | solution.py:51
  155.1 8.8 %all-to-all-start.6 = ((f32[8,1,4096]{2,1,0:T(1,128)}), f32[8,1,4096]{2,1,0:T(1,128)S(1)}, u32[]{:S(2)}, u32[]{:S(2)}) async-start(f32[8,1,4096]{2,1,0:T(1,128)} %copy.63), calls=%async_computation.6 | async-start | bytes 262144 | tf_op jit(solution)/shard_map/all_to_all | solution.py:51
Sparse Core Ops, SparseCore 0:
  24.2 45.6 all-gather.2
  71.4 44.4 all-gather.4
where the time goes:
time: 173 us; the launch traced here: 172 us
  waiting for transfers between devices  81.8 us (47%)
  blocking collectives  35.1 us (20%)
  starting transfers between devices  20.7 us (12%)
  between operations  14.3 us (8%)
  local copies, waits for them, and re-layouts  14.2 us (8%)
  other arithmetic  3.18 us (2%)
  matrix products  2.77 us (2%)
    all_gather x2, waiting for transfers between devices, body(): kv_block = lax.all_gather(moved_layer, 'rep', axis=2, tiled=True)  57.7 us
    all_to_all x2, blocking collectives, body(): lax.all_to_all(prefix_cache[layer_index], 'seq', split_axis=2, concat_axi...  26.8 us
    all_to_all x2, waiting for transfers between devices, body(): lax.all_to_all(numerator, 'seq', split_axis=0, concat_axis=1, tiled=True)  10.3 us
    all_to_all x2, waiting for transfers between devices, body(): lax.all_to_all(denominator, 'seq', split_axis=0, concat_axis=1, tiled=True)  9.17 us
    all_gather x1, blocking collectives, body(): gathered = lax.all_gather(queries, 'seq', axis=1, tiled=True)  8.25 us
    all_to_all x2, starting transfers between devices, body(): lax.all_to_all(source_tops, 'seq', split_axis=0, concat_axis=1, tiled=True)  7.31 us
    all_to_all x2, starting transfers between devices, body(): lax.all_to_all(numerator, 'seq', split_axis=0, concat_axis=1, tiled=True)  6.74 us
    all_to_all x2, starting transfers between devices, body(): lax.all_to_all(denominator, 'seq', split_axis=0, concat_axis=1, tiled=True)  6.59 us
  transfers between devices with their start and end apart: 8, of which 7 were waited for; matrix products, arithmetic and copies ran while one was open for 9% of the time, Pallas kernels for 0%

commit v1 on v0

v1 whole, which is shorter than its diff:
```python
import functools

import jax
import jax.numpy as jnp
from jax import lax
from jax.experimental import pallas as pl
from jax.experimental.pallas import tpu as pltpu
from jax.sharding import PartitionSpec as P

QH = 32
KVH = 8
HD = 128
GROUP = QH // KVH
neg_fill = -1e30
LOG2E = 1.4426950408889634
SCALE = HD ** -0.5 * LOG2E
CHUNK = 32
NT = (((1,), (1,)), ((), ()))


def layer_rows(shape, layers):
    return (lax.broadcasted_iota(jnp.int32, shape, 0) // GROUP) % layers


def kernel(
    n_rep, n_all, span, layers,
    lengths_ref, slot_ref, cache_ref, q_ref, suffix_ref, out_ref,
    kv, sfx, q_row, q_f32, q_send, q_recv, o_send, o_recv,
    load_sem, q_send_sem, q_recv_sem, o_send_sem, o_recv_sem,
):
    rows = layers * GROUP
    me_seq = lax.axis_index("seq")
    me_rep = lax.axis_index("rep")
    me = me_seq * n_rep + me_rep

    def place(k):
        other = lax.rem(me + k, n_all)
        return other, {"seq": other // n_rep, "rep": lax.rem(other, n_rep)}

    load_q = pltpu.make_async_copy(q_ref, q_row, load_sem.at[0])
    load_q.start()
    load_sfx = pltpu.make_async_copy(suffix_ref, sfx, load_sem.at[1])
    load_sfx.start()
    load_kv = pltpu.make_async_copy(cache_ref, kv, load_sem.at[2])
    load_kv.start()

    barrier = pltpu.get_barrier_semaphore()

    @pl.loop(1, n_all)
    def _(k):
        _, where = place(k)
        pl.semaphore_signal(barrier, inc=1, device_id=where, device_id_type=pl.DeviceIdType.MESH)

    load_q.wait()
    for l in range(layers):
        for k in range(QH):
            h, g = k // GROUP, k % GROUP
            q_f32[h, l * GROUP + g : l * GROUP + g + 1, :] = q_row[
                l, :, k * HD : (k + 1) * HD
            ].astype(jnp.float32)
    q_send[...] = q_f32[...].astype(jnp.bfloat16)

    pl.semaphore_wait(barrier, n_all - 1)

    my_head = me_seq // span
    own_q = pltpu.make_async_copy(q_send.at[my_head], q_recv.at[me], q_recv_sem)
    own_q.start()

    @pl.loop(1, n_all)
    def _(k):
        other, where = place(k)
        pltpu.make_async_remote_copy(
            src_ref=q_send.at[other // n_rep // span],
            dst_ref=q_recv.at[me],
            send_sem=q_send_sem,
            recv_sem=q_recv_sem,
            device_id=where,
            device_id_type=pl.DeviceIdType.MESH,
        ).start()

    load_sfx.wait()
    s_rows = KVH * rows
    length = lengths_ref[slot_ref[0]]
    q_all = q_f32[...].reshape(s_rows, HD)
    head_of = lax.broadcasted_iota(jnp.int32, (s_rows, HD), 0) // rows
    q_diag = jnp.concatenate(
        [jnp.where(head_of == h, q_all, 0.0) for h in range(KVH)], axis=1
    ).astype(jnp.bfloat16)
    suf = sfx.shape[3]
    lay_s = layer_rows((s_rows, suf), layers)
    scores = jnp.zeros((s_rows, suf), jnp.float32)
    for l in range(layers):
        part = lax.dot_general(q_diag, sfx[l, 0, 0], NT, preferred_element_type=jnp.float32)
        scores = jnp.where(lay_s == l, part, scores)
    valid = lax.broadcasted_iota(jnp.int32, (s_rows, suf), 1) < length
    scores = jnp.where(valid, scores * SCALE, neg_fill)
    s_top = jnp.max(scores, axis=1, keepdims=True)
    s_w = jnp.where(valid, jnp.exp2(scores - s_top), 0.0).astype(jnp.bfloat16)
    s_den = jnp.sum(s_w.astype(jnp.float32), axis=1, keepdims=True)
    lay_h = layer_rows((s_rows, HD), layers)
    s_num = jnp.zeros((s_rows, HD), jnp.float32)
    for l in range(layers):
        part = jnp.dot(s_w, sfx[l, 0, 1], preferred_element_type=jnp.float32)
        for h in range(KVH):
            s_num = jnp.where(
                (head_of == h) & (lay_h == l), part[:, h * HD : (h + 1) * HD], s_num
            )

    load_kv.wait()
    pltpu.make_async_copy(q_recv, q_recv, q_recv_sem).wait()

    chunk = min(CHUNK, n_all)
    c_rows = chunk * rows
    positions = kv.shape[3]

    def one_chunk(base):
        q_c = q_recv[pl.ds(base, chunk)].astype(jnp.float32).reshape(c_rows, HD)
        lay = layer_rows((c_rows, HD), layers)
        q_c = jnp.concatenate(
            [jnp.where(lay == l, q_c, 0.0) for l in range(layers)], axis=1
        ).astype(jnp.bfloat16)
        keys = kv[:, 0].reshape(layers * HD, positions)
        values = kv[:, 1].reshape(layers * HD, positions)
        s = jnp.dot(q_c, keys, preferred_element_type=jnp.float32) * SCALE
        top = jnp.max(s, axis=1, keepdims=True)
        w = jnp.exp2(s - top).astype(jnp.bfloat16)
        den = jnp.sum(w.astype(jnp.float32), axis=1, keepdims=True)
        num_all = lax.dot_general(w, values, NT, preferred_element_type=jnp.float32)
        num = num_all[:, :HD]
        for l in range(1, layers):
            num = jnp.where(lay == l, num_all[:, l * HD : (l + 1) * HD], num)
        lse = top + jnp.log2(den)
        high = lse.astype(jnp.bfloat16).astype(jnp.float32)
        mid = (lse - high).astype(jnp.bfloat16).astype(jnp.float32)
        low = lse - high - mid
        lane = lax.broadcasted_iota(jnp.int32, (c_rows, HD), 1)
        stat = jnp.where(lane == 0, high, jnp.where(lane == 1, mid, jnp.where(lane == 2, low, 0.0)))
        both = jnp.concatenate(
            [(num / den).reshape(chunk, rows, HD), stat.reshape(chunk, rows, HD)], axis=1
        )
        o_send[pl.ds(base, chunk)] = both.astype(jnp.bfloat16)

    if chunk == n_all:
        one_chunk(0)
    else:
        @pl.loop(0, n_all // chunk)
        def _(c):
            one_chunk(c * chunk)

    own_o = pltpu.make_async_copy(o_send.at[me], o_recv.at[me], o_recv_sem)
    own_o.start()

    @pl.loop(1, n_all)
    def _(k):
        other, where = place(k)
        pltpu.make_async_remote_copy(
            src_ref=o_send.at[other],
            dst_ref=o_recv.at[me],
            send_sem=o_send_sem,
            recv_sem=o_recv_sem,
            device_id=where,
            device_id_type=pl.DeviceIdType.MESH,
        ).start()

    s_out = (s_num / s_den).reshape(KVH, rows, HD)
    s_lse = (s_top + jnp.log2(s_den)).reshape(KVH, rows, 1)
    others = pl.ds(0, n_all - 1)
    sent_q = q_recv.at[others]
    pltpu.make_async_copy(sent_q, sent_q, q_send_sem).wait()
    pltpu.make_async_copy(o_recv, o_recv, o_recv_sem).wait()

    per_head = n_all // KVH
    for h in range(KVH):
        got = o_recv[h * per_head : (h + 1) * per_head].astype(jnp.float32)
        part = got[:, :rows]
        lse = jnp.sum(got[:, rows:], axis=2, keepdims=True)
        top = jnp.maximum(jnp.max(lse, axis=0), s_lse[h])
        wgt = jnp.exp2(lse - top[None])
        s_wgt = jnp.exp2(s_lse[h] - top)
        num = jnp.sum(wgt * part, axis=0) + s_wgt * s_out[h]
        den = jnp.sum(wgt, axis=0) + s_wgt
        mixed = num / den
        for l in range(layers):
            for g in range(GROUP):
                at = (h * GROUP + g) * HD
                r = l * GROUP + g
                out_ref[l, :, at : at + HD] = mixed[r : r + 1].astype(out_ref.dtype)

    sent_o = o_recv.at[others]
    pltpu.make_async_copy(sent_o, sent_o, o_send_sem).wait()


def attend(n_seq, n_rep, prefix_cache, queries, suffix_cache, suffix_lengths, slot_request):
    layers, _, width = queries.shape
    n_all = n_seq * n_rep
    features = prefix_cache.shape[2]
    span = HD // features
    if span > 1:
        groups = [[h * span + j for j in range(span)] for h in range(n_seq // span)]
        prefix_cache = lax.all_to_all(
            prefix_cache, "seq", split_axis=3, concat_axis=2, axis_index_groups=groups, tiled=True
        )
    rows = layers * GROUP
    any_spec = pl.BlockSpec(memory_space=pl.ANY)
    smem_spec = pl.BlockSpec(memory_space=pltpu.SMEM)
    return pl.pallas_call(
        functools.partial(kernel, n_rep, n_all, span, layers),
        out_shape=jax.ShapeDtypeStruct(queries.shape, queries.dtype),
        in_specs=[smem_spec, smem_spec, any_spec, any_spec, any_spec],
        out_specs=pl.BlockSpec(memory_space=pltpu.VMEM),
        scratch_shapes=[
            pltpu.VMEM(prefix_cache.shape, jnp.bfloat16),
            pltpu.VMEM(suffix_cache.shape, jnp.bfloat16),
            pltpu.VMEM(queries.shape, jnp.bfloat16),
            pltpu.VMEM((KVH, rows, HD), jnp.float32),
            pltpu.VMEM((KVH, rows, HD), jnp.bfloat16),
            pltpu.VMEM((n_all, rows, HD), jnp.bfloat16),
            pltpu.VMEM((n_all, 2 * rows, HD), jnp.bfloat16),
            pltpu.VMEM((n_all, 2 * rows, HD), jnp.bfloat16),
            pltpu.SemaphoreType.DMA((3,)),
            pltpu.SemaphoreType.DMA,
            pltpu.SemaphoreType.DMA,
            pltpu.SemaphoreType.DMA,
            pltpu.SemaphoreType.DMA,
        ],
        compiler_params=pltpu.CompilerParams(collective_id=0, has_side_effects=True),
    )(suffix_lengths, slot_request, prefix_cache, queries, suffix_cache)


def solution(mesh):
    in_specs = (
        P(None, None, "seq", "rep"),
        P(None, ("seq", "rep"), None),
        P(None, ("seq", "rep"), None, None, None),
        P(),
        P(("seq", "rep")),
    )
    return jax.shard_map(
        functools.partial(attend, mesh.shape["seq"], mesh.shape["rep"]),
        mesh=mesh,
        in_specs=in_specs,
        out_specs=P(None, ("seq", "rep"), None),
        check_vma=False,
    )
```

time: 173 us -> 22.9 us (0.13)
  waiting for transfers between devices: 81.8 us -> 0 us
  blocking collectives: 35.1 us -> 0 us
  starting transfers between devices: 20.7 us -> 0 us
  Pallas kernels: 0 us -> 19.2 us
  between operations: 14.3 us -> 0.66 us
  local copies, waits for them, and re-layouts: 14.2 us -> 2.73 us
  other arithmetic: 3.18 us -> 0 us
  matrix products: 2.77 us -> 0 us
    all_gather x2 -> x0, waiting for transfers between devices: 57.7 us -> none  [body(): kv_block = lax.all_gather(moved_layer, 'rep', axis=2, tiled=True)]
    all_to_all x2 -> x0, blocking collectives: 26.8 us -> none  [body(): lax.all_to_all(prefix_cache[layer_index], 'seq', split_axis=2, concat_axi...]
    all_to_all x6 -> x0, waiting for transfers between devices: 24 us -> none  [the longest x2 10.3 us: body(): lax.all_to_all(numerator, 'seq', split_axis=0, concat_axis=1, tiled=True)]
    all_to_all x6 -> x0, starting transfers between devices: 20.6 us -> none  [the longest x2 7.31 us: body(): lax.all_to_all(source_tops, 'seq', split_axis=0, concat_axis=1, tiled=True)]
    pallas_call x0 -> x1, Pallas kernels: none -> 19.2 us  [attend(): pl.pallas_call(functools.partial(kernel, n_rep, n_all, span, layers), out...]
    all_gather x1 -> x0, blocking collectives: 8.25 us -> none  [body(): gathered = lax.all_gather(queries, 'seq', axis=1, tiled=True)]
    slice x6 -> x0, local copies, waits for them, and re-layouts: 5.34 us -> none  [the longest x2 3.35 us: body(): value_block = kv_block[1].reshape(KVH, HD, positions)]
    reshape x10 -> x0, local copies, waits for them, and re-layouts: 4.54 us -> none  [the longest x2 1.56 us: body(): numerator = jnp.einsum('rhgp,hdp->rhgd', weights, value_block, preferred_...]
  transfers between devices with their start and end apart: 8 -> 0, of which waited for: 7 -> 0; matrix products, arithmetic and copies ran while one was open for 9% -> 0% of each run, Pallas kernels for 0% -> 0%
where the time goes in v1:
time: 22.9 us; the launch traced here: 22.6 us
  Pallas kernels  19.2 us (84%)
  local copies, waits for them, and re-layouts  2.73 us (12%)
  between operations  0.66 us (3%)
    pallas_call x1, Pallas kernels, attend(): pl.pallas_call(functools.partial(kernel, n_rep, n_all, span, layers), out...  19.2 us
    pallas_call x1, local copies, waits for them, and re-layouts, attend(): pl.pallas_call(functools.partial(kernel, n_rep, n_all, span, layers), out...  1.39 us
    unnamed x1, local copies, waits for them, and re-layouts  1.34 us

profile of v1, /device:TPU:0, one launch (start us, length us, event | category | flops | bytes accessed | tf_op | source)
XLA Modules:
  0.0 22.6 jit_solution(12550375754802597385)
XLA Ops:
  0.7 1.3 %copy.6.q_ref = bf16[2,1,4096]{2,1,0:T(2,128)(2,1)} copy(bf16[2,1,4096]{2,0,1:T(2,128)(2,1)} %param.6) | data formatting | bytes 32768 | tf_op args[1]
  2.0 19.2 %shard_map.55 = bf16[2,1,4096]{2,1,0:T(2,128)(2,1)} custom-call(s32[32]{0:T(128)} %lengths_ref.1, s32[1]{0:T(128)S(6)} %copy.8.slot_ref, bf16[2,2,128,1024]{3,2,1,0:T(8,128)(2,1)} %cache_ref.1, bf16[2,1,4096]{2,1,0:T(2,128)(2,1)} %copy.6.q_ref, bf16[2,1,2,128,1024]{4,3,2,1,0:T(8,128)(2,1)} %suffix_ref.1), custom_call_target="tpu_custom_call" | custom-call | tf_op jit(solution)/shard_map/pallas_call | solution.py:206
  21.2 1.4 %copy.7 = bf16[2,1,4096]{2,0,1:T(2,128)(2,1)} copy(bf16[2,1,4096]{2,1,0:T(2,128)(2,1)} %shard_map.55) | data formatting | bytes 32768 | tf_op jit(solution)/shard_map/pallas_call | solution.py:206

commit v2 on v1

--- a/solution.py
+++ b/solution.py
@@ -25,7 +25,7 @@
 def kernel(
     n_rep, n_all, span, layers,
     lengths_ref, slot_ref, cache_ref, q_ref, suffix_ref, out_ref,
-    kv, sfx, q_row, q_f32, q_send, q_recv, o_send, o_recv,
+    kv, sfx, q_row, q_f32, q_send, q_recv, o_send, o_recv, lengths, slot,
     load_sem, q_send_sem, q_recv_sem, o_send_sem, o_recv_sem,
 ):
     rows = layers * GROUP
@@ -39,6 +39,10 @@
 
     load_q = pltpu.make_async_copy(q_ref, q_row, load_sem.at[0])
     load_q.start()
+    load_len = pltpu.make_async_copy(lengths_ref, lengths, load_sem.at[3])
+    load_len.start()
+    load_slot = pltpu.make_async_copy(slot_ref, slot, load_sem.at[4])
+    load_slot.start()
     load_sfx = pltpu.make_async_copy(suffix_ref, sfx, load_sem.at[1])
     load_sfx.start()
     load_kv = pltpu.make_async_copy(cache_ref, kv, load_sem.at[2])
@@ -56,7 +60,7 @@
         for k in range(QH):
             h, g = k // GROUP, k % GROUP
             q_f32[h, l * GROUP + g : l * GROUP + g + 1, :] = q_row[
-                l, :, k * HD : (k + 1) * HD
+                l : l + 1, k * HD : (k + 1) * HD
             ].astype(jnp.float32)
     q_send[...] = q_f32[...].astype(jnp.bfloat16)
 
@@ -80,7 +84,9 @@
 
     load_sfx.wait()
     s_rows = KVH * rows
-    length = lengths_ref[slot_ref[0]]
+    load_len.wait()
+    load_slot.wait()
+    length = lengths[slot[0]]
     q_all = q_f32[...].reshape(s_rows, HD)
     head_of = lax.broadcasted_iota(jnp.int32, (s_rows, HD), 0) // rows
     q_diag = jnp.concatenate(
@@ -184,7 +190,7 @@
             for g in range(GROUP):
                 at = (h * GROUP + g) * HD
                 r = l * GROUP + g
-                out_ref[l, :, at : at + HD] = mixed[r : r + 1].astype(out_ref.dtype)
+                out_ref[l : l + 1, at : at + HD] = mixed[r : r + 1].astype(out_ref.dtype)
 
     sent_o = o_recv.at[others]
     pltpu.make_async_copy(sent_o, sent_o, o_send_sem).wait()
@@ -201,12 +207,12 @@
             prefix_cache, "seq", split_axis=3, concat_axis=2, axis_index_groups=groups, tiled=True
         )
     rows = layers * GROUP
-    any_spec = pl.BlockSpec(memory_space=pl.ANY)
-    smem_spec = pl.BlockSpec(memory_space=pltpu.SMEM)
-    return pl.pallas_call(
+    any_spec = pl.BlockSpec(memory_space=pltpu.HBM)
+    queries = queries.reshape(layers, width)
+    out = pl.pallas_call(
         functools.partial(kernel, n_rep, n_all, span, layers),
         out_shape=jax.ShapeDtypeStruct(queries.shape, queries.dtype),
-        in_specs=[smem_spec, smem_spec, any_spec, any_spec, any_spec],
+        in_specs=[any_spec, any_spec, any_spec, any_spec, any_spec],
         out_specs=pl.BlockSpec(memory_space=pltpu.VMEM),
         scratch_shapes=[
             pltpu.VMEM(prefix_cache.shape, jnp.bfloat16),
@@ -217,7 +223,9 @@
             pltpu.VMEM((n_all, rows, HD), jnp.bfloat16),
             pltpu.VMEM((n_all, 2 * rows, HD), jnp.bfloat16),
             pltpu.VMEM((n_all, 2 * rows, HD), jnp.bfloat16),
-            pltpu.SemaphoreType.DMA((3,)),
+            pltpu.SMEM(suffix_lengths.shape, jnp.int32),
+            pltpu.SMEM(slot_request.shape, jnp.int32),
+            pltpu.SemaphoreType.DMA((5,)),
             pltpu.SemaphoreType.DMA,
             pltpu.SemaphoreType.DMA,
             pltpu.SemaphoreType.DMA,
@@ -225,6 +233,7 @@
         ],
         compiler_params=pltpu.CompilerParams(collective_id=0, has_side_effects=True),
     )(suffix_lengths, slot_request, prefix_cache, queries, suffix_cache)
+    return out.reshape(layers, 1, width)
 
 
 def solution(mesh):

time: 22.9 us -> 20.9 us (0.913)
  local copies, waits for them, and re-layouts: 2.73 us -> 1.34 us
  Pallas kernels: 19.2 us -> 18.6 us
    pallas_call x1 -> x0, local copies, waits for them, and re-layouts: 1.39 us -> none  [attend(): pl.pallas_call(functools.partial(kernel, n_rep, n_all, span, layers), out...]
    pallas_call x1, Pallas kernels: 19.2 us -> 18.6 us  [attend(): pl.pallas_call(functools.partial(kernel, n_rep, n_all, span, layers), out...]
where the time goes in v2:
time: 20.9 us; the launch traced here: 20.6 us
  Pallas kernels  18.6 us (89%)
  local copies, waits for them, and re-layouts  1.34 us (6%)
  between operations  0.66 us (3%)
    pallas_call x1, Pallas kernels, attend(): pl.pallas_call(functools.partial(kernel, n_rep, n_all, span, layers), out...  18.6 us
    unnamed x1, local copies, waits for them, and re-layouts  1.34 us

profile of v2, /device:TPU:0, one launch (start us, length us, event | category | flops | bytes accessed | tf_op | source)
XLA Modules:
  0.0 20.6 jit_solution(15398242637785391242)
XLA Ops:
  0.7 18.6 %shard_map.55 = bf16[2,4096]{1,0:T(2,128)(2,1)} custom-call(s32[32]{0:T(128)} %lengths_ref.1, s32[1]{0:T(128)S(6)} %copy.7.slot_ref, bf16[2,2,128,1024]{3,2,1,0:T(8,128)(2,1)} %cache_ref.1, bf16[2,4096]{1,0:T(2,128)(2,1)} %bitcast.3, bf16[2,1,2,128,1024]{4,3,2,1,0:T(8,128)(2,1)} %suffix_ref.1), custom_call_target="tpu_custom_call" | custom-call | tf_op jit(solution)/shard_map/pallas_call | solution.py:212
  19.3 1.3 %copy.8 = bf16[2,1,4096]{2,0,1:T(2,128)(2,1)} copy(bf16[2,1,4096]{2,0,1:T(2,128)(2,1)} %bitcast.2) | data formatting | bytes 32768

commit v3 on v2

--- a/solution.py
+++ b/solution.py
@@ -15,11 +15,27 @@
 LOG2E = 1.4426950408889634
 SCALE = HD ** -0.5 * LOG2E
 CHUNK = 32
+UNROLLED = 64
 NT = (((1,), (1,)), ((), ()))
 
 
 def layer_rows(shape, layers):
     return (lax.broadcasted_iota(jnp.int32, shape, 0) // GROUP) % layers
+
+
+def hops(bits):
+    return bits[1] + bin(bits[0] // 2).count("1")
+
+
+def flip(x, bits, size):
+    if size & (size - 1):
+        return lax.rem(x + bits, size)
+    step = 1
+    while step < size:
+        if bits & step:
+            x = x + step - 2 * step * ((x // step) % 2)
+        step *= 2
+    return x
 
 
 def kernel(
@@ -33,9 +49,20 @@
     me_rep = lax.axis_index("rep")
     me = me_seq * n_rep + me_rep
 
-    def place(k):
-        other = lax.rem(me + k, n_all)
-        return other, {"seq": other // n_rep, "rep": lax.rem(other, n_rep)}
+    n_seq = n_all // n_rep
+
+    def each_partner(act):
+        if n_all > UNROLLED:
+            @pl.loop(1, n_all)
+            def _(k):
+                other = lax.rem(me + k, n_all)
+                act(other, {"seq": other // n_rep, "rep": lax.rem(other, n_rep)})
+        else:
+            for bits_seq, bits_rep in sorted(((e, d) for d in range(n_rep) for e in range(n_seq)), key=hops, reverse=True):
+                if bits_seq or bits_rep:
+                    to_seq = flip(me_seq, bits_seq, n_seq)
+                    to_rep = flip(me_rep, bits_rep, n_rep)
+                    act(to_seq * n_rep + to_rep, {"seq": to_seq, "rep": to_rep})
 
     load_q = pltpu.make_async_copy(q_ref, q_row, load_sem.at[0])
     load_q.start()
@@ -50,9 +77,8 @@
 
     barrier = pltpu.get_barrier_semaphore()
 
-    @pl.loop(1, n_all)
-    def _(k):
-        _, where = place(k)
+    @each_partner
+    def _(_, where):
         pl.semaphore_signal(barrier, inc=1, device_id=where, device_id_type=pl.DeviceIdType.MESH)
 
     load_q.wait()
@@ -70,9 +96,8 @@
     own_q = pltpu.make_async_copy(q_send.at[my_head], q_recv.at[me], q_recv_sem)
     own_q.start()
 
-    @pl.loop(1, n_all)
-    def _(k):
-        other, where = place(k)
+    @each_partner
+    def _(other, where):
         pltpu.make_async_remote_copy(
             src_ref=q_send.at[other // n_rep // span],
             dst_ref=q_recv.at[me],
@@ -156,9 +181,8 @@
     own_o = pltpu.make_async_copy(o_send.at[me], o_recv.at[me], o_recv_sem)
     own_o.start()
 
-    @pl.loop(1, n_all)
-    def _(k):
-        other, where = place(k)
+    @each_partner
+    def _(other, where):
         pltpu.make_async_remote_copy(
             src_ref=o_send.at[other],
             dst_ref=o_recv.at[me],
@@ -211,7 +235,7 @@
     queries = queries.reshape(layers, width)
     out = pl.pallas_call(
         functools.partial(kernel, n_rep, n_all, span, layers),
-        out_shape=jax.ShapeDtypeStruct(queries.shape, queries.dtype),
+        out_shape=pltpu.VMEM(queries.shape, queries.dtype),
         in_specs=[any_spec, any_spec, any_spec, any_spec, any_spec],
         out_specs=pl.BlockSpec(memory_space=pltpu.VMEM),
         scratch_shapes=[

time: 20.9 us -> 18.5 us (0.89)
  Pallas kernels: 18.6 us -> 17 us
  local copies, waits for them, and re-layouts: 1.34 us -> 0.61 us
    pallas_call x1, Pallas kernels: 18.6 us -> 17 us  [attend(): pl.pallas_call(functools.partial(kernel, n_rep, n_all, span, layers), out...]
    unnamed x1, local copies, waits for them, and re-layouts: 1.34 us -> 0.61 us
where the time goes in v3:
time: 18.5 us; the launch traced here: 18.3 us
  Pallas kernels  17 us (92%)
  between operations  0.66 us (4%)
  local copies, waits for them, and re-layouts  0.61 us (3%)
    pallas_call x1, Pallas kernels, attend(): pl.pallas_call(functools.partial(kernel, n_rep, n_all, span, layers), out...  17 us
    unnamed x1, local copies, waits for them, and re-layouts  0.61 us

profile of v3, /device:TPU:0, one launch (start us, length us, event | category | flops | bytes accessed | tf_op | source)
XLA Modules:
  0.0 18.3 jit_solution(11264556732557428794)
XLA Ops:
  0.7 17.0 %shard_map.55 = bf16[2,4096]{1,0:T(2,128)(2,1)S(1)} custom-call(s32[32]{0:T(128)} %lengths_ref.1, s32[1]{0:T(128)S(6)} %copy.8.slot_ref, bf16[2,2,128,1024]{3,2,1,0:T(8,128)(2,1)} %cache_ref.1, bf16[2,4096]{1,0:T(2,128)(2,1)} %bitcast.3, bf16[2,1,2,128,1024]{4,3,2,1,0:T(8,128)(2,1)} %suffix_ref.1), custom_call_target="tpu_custom_call" | custom-call | tf_op jit(solution)/shard_map/pallas_call | solution.py:236
  17.7 0.6 %copy.7 = bf16[2,1,4096]{2,0,1:T(2,128)(2,1)} copy(bf16[2,1,4096]{2,0,1:T(2,128)(2,1)S(1)} %bitcast.2) | data formatting | bytes 32768

commit v4 on v2

--- a/solution.py
+++ b/solution.py
@@ -15,11 +15,25 @@
 LOG2E = 1.4426950408889634
 SCALE = HD ** -0.5 * LOG2E
 CHUNK = 32
+UNROLLED = 8
 NT = (((1,), (1,)), ((), ()))
 
 
 def layer_rows(shape, layers):
     return (lax.broadcasted_iota(jnp.int32, shape, 0) // GROUP) % layers
+
+
+def flip(x, bits):
+    step = 1
+    while step <= bits:
+        if bits & step:
+            x = x + step - 2 * step * ((x // step) % 2)
+        step *= 2
+    return x
+
+
+def hops(bits):
+    return bits[1] + bin(bits[0] // 2).count("1")
 
 
 def kernel(
@@ -31,11 +45,24 @@
     rows = layers * GROUP
     me_seq = lax.axis_index("seq")
     me_rep = lax.axis_index("rep")
-    me = me_seq * n_rep + me_rep
-
-    def place(k):
-        other = lax.rem(me + k, n_all)
-        return other, {"seq": other // n_rep, "rep": lax.rem(other, n_rep)}
+
+    n_seq = n_all // n_rep
+
+    def each_partner(distances):
+        def run(act):
+            if n_seq > UNROLLED:
+                for d in distances:
+                    to_rep = flip(me_rep, d)
+
+                    @pl.loop(0 if d else 1, n_seq)
+                    def _(e):
+                        act(lax.rem(me_seq + e, n_seq), to_rep, d)
+            else:
+                pairs = [(e, d) for d in distances for e in range(n_seq) if e or d]
+                for e, d in sorted(pairs, key=hops, reverse=True):
+                    act(flip(me_seq, e), flip(me_rep, d), d)
+
+        return run
 
     load_q = pltpu.make_async_copy(q_ref, q_row, load_sem.at[0])
     load_q.start()
@@ -50,9 +77,9 @@
 
     barrier = pltpu.get_barrier_semaphore()
 
-    @pl.loop(1, n_all)
-    def _(k):
-        _, where = place(k)
+    @each_partner(range(n_rep))
+    def _(to_seq, to_rep, d):
+        where = {"seq": to_seq, "rep": to_rep}
         pl.semaphore_signal(barrier, inc=1, device_id=where, device_id_type=pl.DeviceIdType.MESH)
 
     load_q.wait()
@@ -67,18 +94,21 @@
     pl.semaphore_wait(barrier, n_all - 1)
 
     my_head = me_seq // span
-    own_q = pltpu.make_async_copy(q_send.at[my_head], q_recv.at[me], q_recv_sem)
+    splits = [[d] for d in range(n_rep)]
+    group_of = {d: i for i, group in enumerate(splits) for d in group}
+    own_q = pltpu.make_async_copy(
+        q_send.at[my_head], q_recv.at[0, me_seq], q_recv_sem.at[group_of[0]]
+    )
     own_q.start()
 
-    @pl.loop(1, n_all)
-    def _(k):
-        other, where = place(k)
+    @each_partner(range(n_rep))
+    def _(to_seq, to_rep, d):
         pltpu.make_async_remote_copy(
-            src_ref=q_send.at[other // n_rep // span],
-            dst_ref=q_recv.at[me],
+            src_ref=q_send.at[to_seq // span],
+            dst_ref=q_recv.at[d, me_seq],
             send_sem=q_send_sem,
-            recv_sem=q_recv_sem,
-            device_id=where,
+            recv_sem=q_recv_sem.at[group_of[d]],
+            device_id={"seq": to_seq, "rep": to_rep},
             device_id_type=pl.DeviceIdType.MESH,
         ).start()
 
@@ -113,14 +143,13 @@
             )
 
     load_kv.wait()
-    pltpu.make_async_copy(q_recv, q_recv, q_recv_sem).wait()
-
-    chunk = min(CHUNK, n_all)
-    c_rows = chunk * rows
+
     positions = kv.shape[3]
 
-    def one_chunk(base):
-        q_c = q_recv[pl.ds(base, chunk)].astype(jnp.float32).reshape(c_rows, HD)
+    def one_chunk(d, base, reps, chunk):
+        c_rows = reps * chunk * rows
+        here = (pl.ds(d, reps), pl.ds(base, chunk))
+        q_c = q_recv[here].astype(jnp.float32).reshape(c_rows, HD)
         lay = layer_rows((c_rows, HD), layers)
         q_c = jnp.concatenate(
             [jnp.where(lay == l, q_c, 0.0) for l in range(layers)], axis=1
@@ -142,42 +171,46 @@
         lane = lax.broadcasted_iota(jnp.int32, (c_rows, HD), 1)
         stat = jnp.where(lane == 0, high, jnp.where(lane == 1, mid, jnp.where(lane == 2, low, 0.0)))
         both = jnp.concatenate(
-            [(num / den).reshape(chunk, rows, HD), stat.reshape(chunk, rows, HD)], axis=1
+            [(num / den).reshape(reps, chunk, rows, HD), stat.reshape(reps, chunk, rows, HD)], axis=2
         )
-        o_send[pl.ds(base, chunk)] = both.astype(jnp.bfloat16)
-
-    if chunk == n_all:
-        one_chunk(0)
-    else:
-        @pl.loop(0, n_all // chunk)
-        def _(c):
-            one_chunk(c * chunk)
-
-    own_o = pltpu.make_async_copy(o_send.at[me], o_recv.at[me], o_recv_sem)
-    own_o.start()
-
-    @pl.loop(1, n_all)
-    def _(k):
-        other, where = place(k)
-        pltpu.make_async_remote_copy(
-            src_ref=o_send.at[other],
-            dst_ref=o_recv.at[me],
-            send_sem=o_send_sem,
-            recv_sem=o_recv_sem,
-            device_id=where,
-            device_id_type=pl.DeviceIdType.MESH,
-        ).start()
+        o_send[here] = both.astype(jnp.bfloat16)
+
+    for i, group in enumerate(splits):
+        landed = q_recv.at[pl.ds(group[0], len(group))]
+        pltpu.make_async_copy(landed, landed, q_recv_sem.at[i]).wait()
+        if n_seq * len(group) <= CHUNK:
+            one_chunk(group[0], 0, len(group), n_seq)
+        else:
+            for d in group:
+                chunk = min(CHUNK, n_seq)
+
+                @pl.loop(0, n_seq // chunk)
+                def _(c, d=d, chunk=chunk):
+                    one_chunk(d, c * chunk, 1, chunk)
+
+        if 0 in group:
+            own_o = pltpu.make_async_copy(o_send.at[0, me_seq], o_recv.at[0, me_seq], o_recv_sem)
+            own_o.start()
+
+        @each_partner(group)
+        def _(to_seq, to_rep, d):
+            pltpu.make_async_remote_copy(
+                src_ref=o_send.at[d, to_seq],
+                dst_ref=o_recv.at[d, me_seq],
+                send_sem=o_send_sem,
+                recv_sem=o_recv_sem,
+                device_id={"seq": to_seq, "rep": to_rep},
+                device_id_type=pl.DeviceIdType.MESH,
+            ).start()
 
     s_out = (s_num / s_den).reshape(KVH, rows, HD)
     s_lse = (s_top + jnp.log2(s_den)).reshape(KVH, rows, 1)
-    others = pl.ds(0, n_all - 1)
-    sent_q = q_recv.at[others]
-    pltpu.make_async_copy(sent_q, sent_q, q_send_sem).wait()
     pltpu.make_async_copy(o_recv, o_recv, o_recv_sem).wait()
 
-    per_head = n_all // KVH
+    per_head = n_seq // KVH
     for h in range(KVH):
-        got = o_recv[h * per_head : (h + 1) * per_head].astype(jnp.float32)
+        got = o_recv[:, h * per_head : (h + 1) * per_head].astype(jnp.float32)
+        got = got.reshape(n_rep * per_head, 2 * rows, HD)
         part = got[:, :rows]
         lse = jnp.sum(got[:, rows:], axis=2, keepdims=True)
         top = jnp.maximum(jnp.max(lse, axis=0), s_lse[h])
@@ -192,8 +225,12 @@
                 r = l * GROUP + g
                 out_ref[l : l + 1, at : at + HD] = mixed[r : r + 1].astype(out_ref.dtype)
 
-    sent_o = o_recv.at[others]
-    pltpu.make_async_copy(sent_o, sent_o, o_send_sem).wait()
+    sent_q = (q_recv.at[pl.ds(0, n_rep - 1)], q_recv.at[n_rep - 1, pl.ds(0, n_seq - 1)])
+    for sent in sent_q:
+        pltpu.make_async_copy(sent, sent, q_send_sem).wait()
+    sent_o = (o_recv.at[pl.ds(0, n_rep - 1)], o_recv.at[n_rep - 1, pl.ds(0, n_seq - 1)])
+    for sent in sent_o:
+        pltpu.make_async_copy(sent, sent, o_send_sem).wait()
 
 
 def attend(n_seq, n_rep, prefix_cache, queries, suffix_cache, suffix_lengths, slot_request):
@@ -211,7 +248,7 @@
     queries = queries.reshape(layers, width)
     out = pl.pallas_call(
         functools.partial(kernel, n_rep, n_all, span, layers),
-        out_shape=jax.ShapeDtypeStruct(queries.shape, queries.dtype),
+        out_shape=pltpu.VMEM(queries.shape, queries.dtype),
         in_specs=[any_spec, any_spec, any_spec, any_spec, any_spec],
         out_specs=pl.BlockSpec(memory_space=pltpu.VMEM),
         scratch_shapes=[
@@ -220,14 +257,14 @@
             pltpu.VMEM(queries.shape, jnp.bfloat16),
             pltpu.VMEM((KVH, rows, HD), jnp.float32),
             pltpu.VMEM((KVH, rows, HD), jnp.bfloat16),
-            pltpu.VMEM((n_all, rows, HD), jnp.bfloat16),
-            pltpu.VMEM((n_all, 2 * rows, HD), jnp.bfloat16),
-            pltpu.VMEM((n_all, 2 * rows, HD), jnp.bfloat16),
+            pltpu.VMEM((n_rep, n_seq, rows, HD), jnp.bfloat16),
+            pltpu.VMEM((n_rep, n_seq, 2 * rows, HD), jnp.bfloat16),
+            pltpu.VMEM((n_rep, n_seq, 2 * rows, HD), jnp.bfloat16),
             pltpu.SMEM(suffix_lengths.shape, jnp.int32),
             pltpu.SMEM(slot_request.shape, jnp.int32),
             pltpu.SemaphoreType.DMA((5,)),
             pltpu.SemaphoreType.DMA,
-            pltpu.SemaphoreType.DMA,
+            pltpu.SemaphoreType.DMA((n_rep,)),
             pltpu.SemaphoreType.DMA,
             pltpu.SemaphoreType.DMA,
         ],

time: 20.9 us -> 18.3 us (0.88)
  Pallas kernels: 18.6 us -> 16.8 us
  local copies, waits for them, and re-layouts: 1.34 us -> 0.61 us
    pallas_call x1, Pallas kernels: 18.6 us -> 16.8 us  [attend(): pl.pallas_call(functools.partial(kernel, n_rep, n_all, span, layers), out...]
    unnamed x1, local copies, waits for them, and re-layouts: 1.34 us -> 0.61 us
where the time goes in v4:
time: 18.3 us; the launch traced here: 18.1 us
  Pallas kernels  16.8 us (92%)
  between operations  0.66 us (4%)
  local copies, waits for them, and re-layouts  0.61 us (3%)
    pallas_call x1, Pallas kernels, attend(): pl.pallas_call(functools.partial(kernel, n_rep, n_all, span, layers), out...  16.8 us
    unnamed x1, local copies, waits for them, and re-layouts  0.61 us

profile of v4, /device:TPU:0, one launch (start us, length us, event | category | flops | bytes accessed | tf_op | source)
XLA Modules:
  0.0 18.1 jit_solution(731581508798635617)
XLA Ops:
  0.7 16.8 %shard_map.55 = bf16[2,4096]{1,0:T(2,128)(2,1)S(1)} custom-call(s32[32]{0:T(128)} %lengths_ref.1, s32[1]{0:T(128)S(6)} %copy.8.slot_ref, bf16[2,2,128,1024]{3,2,1,0:T(8,128)(2,1)} %cache_ref.1, bf16[2,4096]{1,0:T(2,128)(2,1)} %bitcast.3, bf16[2,1,2,128,1024]{4,3,2,1,0:T(8,128)(2,1)} %suffix_ref.1), custom_call_target="tpu_custom_call" | custom-call | tf_op jit(solution)/shard_map/pallas_call | solution.py:249
  17.4 0.6 %copy.7 = bf16[2,1,4096]{2,0,1:T(2,128)(2,1)} copy(bf16[2,1,4096]{2,0,1:T(2,128)(2,1)S(1)} %bitcast.2) | data formatting | bytes 32768

commit v5 on v4

--- a/solution.py
+++ b/solution.py
@@ -39,7 +39,7 @@
 def kernel(
     n_rep, n_all, span, layers,
     lengths_ref, slot_ref, cache_ref, q_ref, suffix_ref, out_ref,
-    kv, sfx, q_row, q_f32, q_send, q_recv, o_send, o_recv, lengths, slot,
+    kv, vt, sfx, q_row, q_f32, q_send, q_recv, o_send, o_recv, lengths, slot,
     load_sem, q_send_sem, q_recv_sem, o_send_sem, o_recv_sem,
 ):
     rows = layers * GROUP
@@ -63,6 +63,13 @@
                     act(flip(me_seq, e), flip(me_rep, d), d)
 
         return run
+
+    barrier = pltpu.get_barrier_semaphore()
+
+    @each_partner(range(n_rep))
+    def _(to_seq, to_rep, d):
+        where = {"seq": to_seq, "rep": to_rep}
+        pl.semaphore_signal(barrier, inc=1, device_id=where, device_id_type=pl.DeviceIdType.MESH)
 
     load_q = pltpu.make_async_copy(q_ref, q_row, load_sem.at[0])
     load_q.start()
@@ -74,13 +81,6 @@
     load_sfx.start()
     load_kv = pltpu.make_async_copy(cache_ref, kv, load_sem.at[2])
     load_kv.start()
-
-    barrier = pltpu.get_barrier_semaphore()
-
-    @each_partner(range(n_rep))
-    def _(to_seq, to_rep, d):
-        where = {"seq": to_seq, "rep": to_rep}
-        pl.semaphore_signal(barrier, inc=1, device_id=where, device_id_type=pl.DeviceIdType.MESH)
 
     load_q.wait()
     for l in range(layers):
@@ -145,6 +145,8 @@
     load_kv.wait()
 
     positions = kv.shape[3]
+    for l in range(layers):
+        vt[:, l * HD : (l + 1) * HD] = kv[l, 1].T
 
     def one_chunk(d, base, reps, chunk):
         c_rows = reps * chunk * rows
@@ -155,12 +157,11 @@
             [jnp.where(lay == l, q_c, 0.0) for l in range(layers)], axis=1
         ).astype(jnp.bfloat16)
         keys = kv[:, 0].reshape(layers * HD, positions)
-        values = kv[:, 1].reshape(layers * HD, positions)
         s = jnp.dot(q_c, keys, preferred_element_type=jnp.float32) * SCALE
         top = jnp.max(s, axis=1, keepdims=True)
         w = jnp.exp2(s - top).astype(jnp.bfloat16)
         den = jnp.sum(w.astype(jnp.float32), axis=1, keepdims=True)
-        num_all = lax.dot_general(w, values, NT, preferred_element_type=jnp.float32)
+        num_all = jnp.dot(w, vt[...], preferred_element_type=jnp.float32)
         num = num_all[:, :HD]
         for l in range(1, layers):
             num = jnp.where(lay == l, num_all[:, l * HD : (l + 1) * HD], num)
@@ -253,6 +254,7 @@
         out_specs=pl.BlockSpec(memory_space=pltpu.VMEM),
         scratch_shapes=[
             pltpu.VMEM(prefix_cache.shape, jnp.bfloat16),
+            pltpu.VMEM((prefix_cache.shape[3], layers * HD), jnp.bfloat16),
             pltpu.VMEM(suffix_cache.shape, jnp.bfloat16),
             pltpu.VMEM(queries.shape, jnp.bfloat16),
             pltpu.VMEM((KVH, rows, HD), jnp.float32),

time: 18.3 us -> 18.3 us (level)
  no operation moved by 1% of the time
where the time goes in v5:
time: 18.3 us; the launch traced here: 18 us
  Pallas kernels  16.8 us (92%)
  between operations  0.66 us (4%)
  local copies, waits for them, and re-layouts  0.61 us (3%)
    pallas_call x1, Pallas kernels, attend(): pl.pallas_call(functools.partial(kernel, n_rep, n_all, span, layers), out...  16.8 us
    unnamed x1, local copies, waits for them, and re-layouts  0.61 us

profile of v5, /device:TPU:0, one launch (start us, length us, event | category | flops | bytes accessed | tf_op | source)
XLA Modules:
  0.0 18.0 jit_solution(5288394374729900289)
XLA Ops:
  0.7 16.8 %shard_map.55 = bf16[2,4096]{1,0:T(2,128)(2,1)S(1)} custom-call(s32[32]{0:T(128)} %lengths_ref.1, s32[1]{0:T(128)S(6)} %copy.8.slot_ref, bf16[2,2,128,1024]{3,2,1,0:T(8,128)(2,1)} %cache_ref.1, bf16[2,4096]{1,0:T(2,128)(2,1)} %bitcast.3, bf16[2,1,2,128,1024]{4,3,2,1,0:T(8,128)(2,1)} %suffix_ref.1), custom_call_target="tpu_custom_call" | custom-call | tf_op jit(solution)/shard_map/pallas_call | solution.py:250
  17.4 0.6 %copy.7 = bf16[2,1,4096]{2,0,1:T(2,128)(2,1)} copy(bf16[2,1,4096]{2,0,1:T(2,128)(2,1)S(1)} %bitcast.2) | data formatting | bytes 32768
